TPU v7x, 256 devices: a whole 4x4x8 slice. The times are simulated.
256 devices in a mesh: section: 2 (over x_hi), feat: 16 (over y, x_lo, core), width: 8 (over z).
Axes of the slice: x: 4 (x_hi: 2, x_lo: 2; x = x_hi * 2 + x_lo), y: 4, z: 8, core: 2. Of those that a mesh axis runs over, the one named last changes fastest.
Arguments:
- mlp_inputs: bfloat16 [4, 1024, 2304], P('section', 'width'), may hold values from -6 to 6
- encoder: bfloat16 [4, 2304, 16384], P('section', 'width', 'feat'), may hold values from -0.125 to 0.125
- enc_bias: float32 [4, 16384], P('section', 'feat'), may hold values from -3 to 3
- decoder: bfloat16 [10, 16384, 2304], P('section', 'feat', 'width'), may hold values from -0.046875 to 0.046875
- dec_bias: float32 [4, 2304], P(None, 'width'), may hold values from -3 to 3
- targets: bfloat16 [4, 1024, 2304], P(None, None, 'width'), may hold values from -6 to 6
- live_rows: int32 [1024], replicated, may hold values 0 or 1
Outputs:
- errors: bfloat16 [4, 1024, 2304], P(None, None, 'width')
- gradients: bfloat16 [10, 16384, 2304], P('section', 'feat', 'width')
All inputs are finite; a program needn't handle non-finite values.
Results may differ from a plain program's by a relative error of at most 0.0042.
Values may be sent and summed in bfloat16 or wider, within the bound.
No kernel may reach another device: no remote copies, remote signals or barrier semaphores. Data moves between devices by JAX's collectives and lax.ppermute only.
A program may use at most 128 MiB of HBM per device.

v0:
```python
import jax
import jax.numpy as jnp
from jax import lax
from jax.sharding import PartitionSpec as P


def from_behind(value, axis, steps):
    count = lax.axis_size(axis)
    initial, last = (max(0, -steps), min(count, count - steps))
    return lax.ppermute(value, axis, [(source, source + steps) for source in range(initial, last)])


def pair_tables(layer_count):
    source_ids = []
    target_ids = []
    for source in range(layer_count):
        for target in range(source, layer_count):
            source_ids.append(source)
            target_ids.append(target)
    return (jnp.array(source_ids, jnp.int32), jnp.array(target_ids, jnp.int32))


def local(mlp_inputs, encoder, enc_bias, decoder, dec_bias, targets, live_rows):
    layers_here, tok_local, model_width = mlp_inputs.shape
    pre_act = jnp.einsum(
        "ltd,ldf->tlf",
        mlp_inputs,
        lax.all_gather(encoder, "width", axis=1, tiled=True),
        preferred_element_type=jnp.float32,
    )
    local_feats = jnp.maximum(pre_act + enc_bias[None, :, :], 0.0).astype(jnp.bfloat16)
    token_feats = lax.all_gather(local_feats, "width", axis=0, tiled=True)
    layers_all = dec_bias.shape[0]
    tokens_all = live_rows.shape[0]
    per_section = decoder.shape[0]
    source_ids, target_ids = pair_tables(layers_all)
    section_id = lax.axis_index("section")
    earlier = from_behind(token_feats[:, layers_here - 1], "section", 1)
    features = jnp.concatenate([earlier[:, None, :], token_feats], axis=1)
    first_layer = section_id * layers_here - 1
    rebuilt = jnp.zeros((layers_all, tokens_all, decoder.shape[2]), jnp.float32)
    chosen = []
    for pair_slot in range(per_section):
        pair_id = section_id * per_section + pair_slot
        source = source_ids[pair_id]
        target = target_ids[pair_id]
        picked = lax.dynamic_index_in_dim(features, source - first_layer, 1, keepdims=False)
        chosen.append((picked, target))
        partial_value = jnp.dot(picked, decoder[pair_slot], preferred_element_type=jnp.float32)
        current = lax.dynamic_index_in_dim(rebuilt, target, 0, keepdims=False)
        rebuilt = lax.dynamic_update_index_in_dim(rebuilt, current + partial_value, target, 0)
    summed = lax.psum(rebuilt, ("section", "feat"))
    keep_rows = live_rows.astype(jnp.float32)[None, :, None]
    errors = ((summed + dec_bias[:, None, :] - targets.astype(jnp.float32)) * keep_rows).astype(
        jnp.bfloat16
    )
    gradients = []
    for picked, target in chosen:
        residual = lax.dynamic_index_in_dim(errors, target, 0, keepdims=False)
        product = lax.dot_general(
            picked, residual, (((0,), (0,)), ((), ())), preferred_element_type=jnp.float32
        )
        gradients.append((product / tokens_all).astype(jnp.bfloat16))
    return (errors, jnp.stack(gradients))


def solution(mesh):
    placed = (
        P("section", "width", None),
        P("section", "width", "feat"),
        P("section", "feat"),
        P("section", "feat", "width"),
        P(None, "width"),
        P(None, None, "width"),
        P(),
    )
    return jax.shard_map(
        local,
        mesh=mesh,
        in_specs=placed,
        out_specs=(P(None, None, "width"), P("section", "feat", "width")),
        check_vma=False,
    )
```

profile of v0, /device:TPU:1, one launch (start us, length us, event | category | flops | bytes accessed | tf_op | source)
XLA Modules:
  0.0 397.8 jit_solution(8431505922366384273)
XLA Ops:
  8.0 109.4 %all-gather.3.cloned.1.call-done = bf16[2,2304,1024]{2,1,0:T(8,128)(2,1)} async-done(((bf16[2,288,1024]{2,1,0:T(8,128)(2,1)}), bf16[2,2304,1024]{2,1,0:T(8,128)(2,1)}) %all-gather.3.cloned.1.call-update) | async-done | bytes 9437200 | tf_op jit(solution)/shard_map/all_gather | solution.py:28
  117.3 7.3 %fusion.36 = bf16[128,2,1024]{0,2,1:T(8,128)(2,1)} fusion(bf16[2,2304,1024]{2,1,0:T(8,128)(2,1)} %all-gather.3.cloned.1.call-done, bf16[2,128,2304]{2,1,0:T(8,128)(2,1)S(1)} %copy-done, f32[2,1024]{1,0:T(2,128)} %param.11), kind=kOutput, calls=%fused_computation.59 | convolution fusion | flops 1208745984 | bytes 11149312 | tf_op jit(solution)/shard_map/ltd,ldf->tlf/dot_general | solution.py:25
  124.7 57.6 %all-gather.5.cloned.1.call-done = bf16[1024,2,1024]{0,2,1:T(8,128)(2,1)} async-done(((bf16[128,2,1024]{0,2,1:T(8,128)(2,1)}), bf16[1024,2,1024]{0,2,1:T(8,128)(2,1)}) %all-gather.5.cloned.1.call-update) | async-done | bytes 4194320 | tf_op jit(solution)/shard_map/all_gather | solution.py:32
  182.4 3.1 slice_bitcast_fusion
  185.4 4.4 %collective-permute-start = (bf16[1024,1024]{0,1:T(8,128)(2,1)}, bf16[1024,1024]{0,1:T(8,128)(2,1)S(1)}, u32[]{:S(2)}, u32[]{:S(2)}) collective-permute-start(bf16[1024,1024]{0,1:T(8,128)(2,1)} %slice_bitcast_fusion), channel_id=1, source_target_pairs={{0,128},{1,129},{2,130},{3,131},{4,132},{5,133},{6,134},{7,135},{8... | collective-permute-start | bytes 6291464 | tf_op jit(solution)/shard_map/ppermute | solution.py:10
  203.2 26.7 %collective-permute-done = bf16[1024,1024]{0,1:T(8,128)(2,1)S(1)} collective-permute-done((bf16[1024,1024]{0,1:T(8,128)(2,1)}, bf16[1024,1024]{0,1:T(8,128)(2,1)S(1)}, u32[]{:S(2)}, u32[]{:S(2)}) %collective-permute-start) | collective-permute-done | bytes 2097184 | tf_op jit(solution)/shard_map/ppermute | solution.py:10
  229.9 3.0 broadcast_in_dim.25
  233.7 3.4 fusion.18
  237.1 1.3 constant_dynamic-slice_fusion.3
  238.5 2.2 fusion.17
  240.7 1.3 constant_dynamic-slice_fusion.2
  242.1 2.2 fusion.15
  244.3 1.3 constant_dynamic-slice_fusion.1
  245.6 2.3 fusion.13
  247.9 1.3 constant_dynamic-slice_fusion
  249.3 2.2 fusion.11
  252.2 126.4 %all-reduce.2.cloned.1.call-done = f32[4,1024,288]{1,2,0:T(8,128)} async-done(((f32[4,1024,288]{1,2,0:T(8,128)}), f32[4,1024,288]{1,2,0:T(8,128)}) %all-reduce.2.cloned.1.call-update) | async-done | bytes 4718608 | tf_op jit(solution)/shard_map/psum | solution.py:52
  378.6 3.9 multiply_convert_fusion
  382.8 1.4 fusion.35
  384.2 1.4 fusion.33
  385.6 1.4 fusion.31
  386.9 1.4 fusion.29
  388.3 1.4 fusion.27
  389.7 1.6 copy-done.9
  (27 shorter events, 3.4 us)
Async XLA Ops:
  7.2 110.2 %copy-start = (bf16[2,128,2304]{2,1,0:T(8,128)(2,1)S(1)}, bf16[2,128,2304]{2,1,0:T(8,128)(2,1)}, u32[]{:S(2)}) copy-start(bf16[2,128,2304]{2,1,0:T(8,128)(2,1)} %param.9) | copy-start | bytes 3538948
  7.2 110.2 %all-gather.3.cloned.1.call-start = ((), (), s32[]{:S(2)}) async-start(), calls=%async_computation | async-start | bytes 10616832 | tf_op jit(solution)/shard_map/all_gather | solution.py:28
  7.9 174.4 %all-gather.5.cloned.1.call-start = ((), (), s32[]{:S(2)}) async-start(), calls=%async_computation.1 | async-start | bytes 4718592 | tf_op jit(solution)/shard_map/all_gather | solution.py:32
  124.7 65.2 %copy-start.5 = (s32[10]{0:T(128)S(1)}, s32[10]{0:T(128)}, u32[]{:S(2)}) copy-start(s32[10]{0:T(128)} %constant.92.clone) | copy-start | bytes 124
  124.7 65.2 %copy-start.6 = (s32[10]{0:T(128)S(1)}, s32[10]{0:T(128)}, u32[]{:S(2)}) copy-start(s32[10]{0:T(128)} %constant.93.clone) | copy-start | bytes 124
  124.7 253.9 %all-reduce.2.cloned.1.call-start = ((), (), s32[]{:S(2)}) async-start(), calls=%async_computation.2 | async-start | bytes 9437184 | tf_op jit(solution)/shard_map/psum | solution.py:52
  185.4 44.5 %collective-permute-start = (bf16[1024,1024]{0,1:T(8,128)(2,1)}, bf16[1024,1024]{0,1:T(8,128)(2,1)S(1)}, u32[]{:S(2)}, u32[]{:S(2)}) collective-permute-start(bf16[1024,1024]{0,1:T(8,128)(2,1)} %slice_bitcast_fusion), channel_id=1, source_target_pairs={{0,128},{1,129},{2,130},{3,131},{4,132},{5,133},{6,134},{7,135},{8... | collective-permute-start | bytes 6291464 | tf_op jit(solution)/shard_map/ppermute | solution.py:10
  229.9 3.8 copy-start.1
  233.7 4.7 %copy-start.3 = (bf16[5,1024,288]{1,2,0:T(8,128)(2,1)S(1)}, bf16[5,1024,288]{1,2,0:T(8,128)(2,1)}, u32[]{:S(2)}) copy-start(bf16[5,1024,288]{1,2,0:T(8,128)(2,1)} %param.12) | copy-start | bytes 8847364
  251.5 0.7 copy-start.8
  251.5 127.1 %copy-start.7 = (f32[4,288]{1,0:T(4,128)S(1)}, f32[4,288]{1,0:T(4,128)}, u32[]{:S(2)}) copy-start(f32[4,288]{1,0:T(4,128)} %param.13) | copy-start | bytes 13828
  378.6 4.2 %copy-start.2 = (bf16[1024,2,1024]{0,2,1:T(8,128)(2,1)S(1)}, bf16[1024,2,1024]{0,2,1:T(8,128)(2,1)}, u32[]{:S(2)}) copy-start(bf16[1024,2,1024]{0,2,1:T(8,128)(2,1)} %all-gather.5.cloned.1.call-done) | copy-start | bytes 12582916
  382.8 5.5 %copy-start.4 = (bf16[4,1024,288]{1,2,0:T(8,128)(2,1)}, bf16[4,1024,288]{1,2,0:T(8,128)(2,1)S(1)}, u32[]{:S(2)}) copy-start(bf16[4,1024,288]{1,2,0:T(8,128)(2,1)S(1)} %multiply_convert_fusion) | copy-start | bytes 7077892
  389.7 1.6 copy-start.9
Sparse Core Ops, SparseCore 0:
  9.8 107.5 all-gather.2
  124.8 57.5 all-gather.4
  251.6 126.9 all-reduce.1
where the time goes:
time: 398 us
  waiting for transfers between devices  321 us (81%)
  matrix products  26.5 us (7%)
  between operations  26.5 us (7%)
  local copies, waits for them, and re-layouts  15.5 us (4%)
  starting transfers between devices  4.52 us (1%)
    psum x1, waiting for transfers between devices, local(): summed = lax.psum(rebuilt, ('section', 'feat'))  126 us
    all_gather x1, waiting for transfers between devices, local(): lax.all_gather(encoder, 'width', axis=1, tiled=True)  109 us
    all_gather x1, waiting for transfers between devices, local(): token_feats = lax.all_gather(local_feats, 'width', axis=0, tiled=True)  57.6 us
    ppermute x1, waiting for transfers between devices, from_behind(): lax.ppermute(value, axis, [(source, source + steps) for source in range(i...  26.7 us
    dot_general x5, matrix products, local(): jnp.dot(picked, decoder[pair_slot], preferred_element_type=jnp.float32)  12.3 us
  transfers between devices with their start and end apart: 4, of which 4 were waited for; matrix products, arithmetic and copies ran while one was open for 0% of the time, Pallas kernels for 0%

commit v1 on v0

--- a/solution.py
+++ b/solution.py
@@ -25,7 +25,9 @@
     pre_act = jnp.einsum(
         "ltd,ldf->tlf",
         mlp_inputs,
-        lax.all_gather(encoder, "width", axis=1, tiled=True),
+        jnp.concatenate(
+            lax.all_to_all(jnp.stack([encoder] * lax.axis_size("width")), "width", 0, 0), axis=1
+        ),
         preferred_element_type=jnp.float32,
     )
     local_feats = jnp.maximum(pre_act + enc_bias[None, :, :], 0.0).astype(jnp.bfloat16)

time: 398 us -> 515 us (1.29)
  blocking collectives: 0 us -> 216 us
  waiting for transfers between devices: 321 us -> 210 us
  local copies, waits for them, and re-layouts: 15.5 us -> 27 us
    all_to_all x0 -> x1, blocking collectives: none -> 216 us  [local(): lax.all_to_all(jnp.stack([encoder] * lax.axis_size('width')), 'width', 0, 0)]
    all_gather x1 -> x0, waiting for transfers between devices: 109 us -> none  [local(): lax.all_gather(encoder, 'width', axis=1, tiled=True)]
    all_to_all x0 -> x1, local copies, waits for them, and re-layouts: none -> 8.87 us  [local(): lax.all_to_all(jnp.stack([encoder] * lax.axis_size('width')), 'width', 0, 0)]
  transfers between devices with their start and end apart: 4 -> 3, of which waited for: 4 -> 3; matrix products, arithmetic and copies ran while one was open for 0% -> 0% of each run, Pallas kernels for 0% -> 0%
where the time goes in v1:
time: 515 us
  blocking collectives  216 us (42%)
  waiting for transfers between devices  210 us (41%)
  local copies, waits for them, and re-layouts  27 us (5%)
  between operations  26.6 us (5%)
  matrix products  26.5 us (5%)
    all_to_all x1, blocking collectives, local(): lax.all_to_all(jnp.stack([encoder] * lax.axis_size('width')), 'width', 0, 0)  216 us
    psum x1, waiting for transfers between devices, local(): summed = lax.psum(rebuilt, ('section', 'feat'))  126 us
    all_gather x1, waiting for transfers between devices, local(): token_feats = lax.all_gather(local_feats, 'width', axis=0, tiled=True)  56.9 us
    ppermute x1, waiting for transfers between devices, from_behind(): lax.ppermute(value, axis, [(source, source + steps) for source in range(i...  26.9 us
    dot_general x5, matrix products, local(): jnp.dot(picked, decoder[pair_slot], preferred_element_type=jnp.float32)  12.4 us
  transfers between devices with their start and end apart: 3, of which 3 were waited for; matrix products, arithmetic and copies ran while one was open for 0% of the time, Pallas kernels for 0%

profile of v1, /device:TPU:1, one launch (start us, length us, event | category | flops | bytes accessed | tf_op | source)
XLA Modules:
  0.0 514.6 jit_solution(520107911801203818)
XLA Ops:
  7.2 2.6 stack.14
  9.8 216.0 %all_to_all.5 = bf16[8,2,288,1024]{3,2,1,0:T(8,128)(2,1)} all-to-all(bf16[8,2,288,1024]{3,2,1,0:T(8,128)(2,1)S(1)} %stack.14), channel_id=1, replica_groups=mesh['section'=2,'feat'=16,'width'=8] {'width'}, dimensions={0} | all-to-all | bytes 18874368 | tf_op jit(solution)/shard_map/all_to_all | solution.py:29
  225.8 8.9 %copy.13 = bf16[8,2,288,1024]{3,2,0,1:T(8,128)(2,1)} copy(bf16[8,2,288,1024]{3,2,1,0:T(8,128)(2,1)} %all_to_all.5) | data formatting | bytes 18874368 | tf_op jit(solution)/shard_map/all_to_all | solution.py:29
  234.7 7.3 %fusion.36 = bf16[128,2,1024]{0,2,1:T(8,128)(2,1)} fusion(bf16[2,2304,1024]{2,1,0:T(8,128)(2,1)} %bitcast.128, bf16[2,128,2304]{2,1,0:T(8,128)(2,1)S(1)} %copy-done, f32[2,1024]{1,0:T(2,128)S(1)} %copy-done.5), kind=kOutput, calls=%fused_computation.59 | convolution fusion | flops 1208745984 | bytes 11149312 | tf_op jit(solution)/shard_map/ltd,ldf->tlf/dot_general | solution.py:25
  242.1 56.9 %all-gather.2.cloned.1.call-done = bf16[1024,2,1024]{0,2,1:T(8,128)(2,1)} async-done(((bf16[128,2,1024]{0,2,1:T(8,128)(2,1)}), bf16[1024,2,1024]{0,2,1:T(8,128)(2,1)}) %all-gather.2.cloned.1.call-update) | async-done | bytes 4194320 | tf_op jit(solution)/shard_map/all_gather | solution.py:34
  298.9 3.1 slice_bitcast_fusion
  302.0 4.4 collective-permute-start
  319.6 26.9 %collective-permute-done = bf16[1024,1024]{0,1:T(8,128)(2,1)S(1)} collective-permute-done((bf16[1024,1024]{0,1:T(8,128)(2,1)}, bf16[1024,1024]{0,1:T(8,128)(2,1)S(1)}, u32[]{:S(2)}, u32[]{:S(2)}) %collective-permute-start) | collective-permute-done | bytes 2097184 | tf_op jit(solution)/shard_map/ppermute | solution.py:10
  346.5 3.0 broadcast_in_dim.25
  350.3 3.4 fusion.18
  353.7 1.3 constant_dynamic-slice_fusion.3
  355.1 2.2 fusion.17
  357.3 1.3 constant_dynamic-slice_fusion.2
  358.7 2.2 fusion.15
  362.2 2.3 fusion.13
  365.9 2.2 fusion.11
  368.8 126.3 %all-reduce.2.cloned.1.call-done = f32[4,1024,288]{1,2,0:T(8,128)} async-done(((f32[4,1024,288]{1,2,0:T(8,128)}), f32[4,1024,288]{1,2,0:T(8,128)}) %all-reduce.2.cloned.1.call-update) | async-done | bytes 4718608 | tf_op jit(solution)/shard_map/psum | solution.py:54
  495.1 3.9 multiply_convert_fusion
  499.3 1.4 fusion.35
  500.7 1.4 fusion.33
  502.1 1.4 fusion.31
  503.4 1.4 fusion.29
  504.8 1.4 fusion.27
  506.2 1.6 copy-done.10
  (29 shorter events, 5.3 us)
Async XLA Ops:
  7.2 227.5 %copy-start = (bf16[2,128,2304]{2,1,0:T(8,128)(2,1)S(1)}, bf16[2,128,2304]{2,1,0:T(8,128)(2,1)}, u32[]{:S(2)}) copy-start(bf16[2,128,2304]{2,1,0:T(8,128)(2,1)} %param.9) | copy-start | bytes 3538948
  7.2 291.8 %all-gather.2.cloned.1.call-start = ((), (), s32[]{:S(2)}) async-start(), calls=%async_computation.1 | async-start | bytes 4718592 | tf_op jit(solution)/shard_map/all_gather | solution.py:34
  225.8 8.9 %copy-start.5 = (f32[2,1024]{1,0:T(2,128)S(1)}, f32[2,1024]{1,0:T(2,128)}, u32[]{:S(2)}) copy-start(f32[2,1024]{1,0:T(2,128)} %param.11) | copy-start | bytes 24580
  242.0 64.4 %copy-start.6 = (s32[10]{0:T(128)S(1)}, s32[10]{0:T(128)}, u32[]{:S(2)}) copy-start(s32[10]{0:T(128)} %constant.92.clone) | copy-start | bytes 124
  242.0 64.4 %copy-start.7 = (s32[10]{0:T(128)S(1)}, s32[10]{0:T(128)}, u32[]{:S(2)}) copy-start(s32[10]{0:T(128)} %constant.93.clone) | copy-start | bytes 124
  242.0 253.0 %all-reduce.2.cloned.1.call-start = ((), (), s32[]{:S(2)}) async-start(), calls=%async_computation.2 | async-start | bytes 9437184 | tf_op jit(solution)/shard_map/psum | solution.py:54
  302.0 44.5 %collective-permute-start = (bf16[1024,1024]{0,1:T(8,128)(2,1)}, bf16[1024,1024]{0,1:T(8,128)(2,1)S(1)}, u32[]{:S(2)}, u32[]{:S(2)}) collective-permute-start(bf16[1024,1024]{0,1:T(8,128)(2,1)} %slice_bitcast_fusion), channel_id=1, source_target_pairs={{0,128},{1,129},{2,130},{3,131},{4,132},{5,133},{6,134},{7,135},{8... | collective-permute-start | bytes 6291464 | tf_op jit(solution)/shard_map/ppermute | solution.py:10
  346.5 3.8 copy-start.1
  350.3 4.7 copy-start.3
  368.1 0.7 copy-start.9
  368.1 127.0 %copy-start.8 = (f32[4,288]{1,0:T(4,128)S(1)}, f32[4,288]{1,0:T(4,128)}, u32[]{:S(2)}) copy-start(f32[4,288]{1,0:T(4,128)} %param.13) | copy-start | bytes 13828
  495.1 4.2 copy-start.2
  499.3 5.5 %copy-start.4 = (bf16[4,1024,288]{1,2,0:T(8,128)(2,1)}, bf16[4,1024,288]{1,2,0:T(8,128)(2,1)S(1)}, u32[]{:S(2)}) copy-start(bf16[4,1024,288]{1,2,0:T(8,128)(2,1)S(1)} %multiply_convert_fusion) | copy-start | bytes 7077892
  506.2 1.6 copy-start.10
Sparse Core Ops, SparseCore 0:
  242.2 56.7 all-gather.1
  368.2 126.7 all-reduce.1
